TPU v7x, 32 devices: a whole 2x2x4 slice. The times are simulated.
32 devices in a mesh: row: 4 (over y, x), col: 8 (over z, core).
Axes of the slice: x: 2, y: 2, z: 4, core: 2. Of those that a mesh axis runs over, the one named last changes fastest.
Arguments:
- pair_states: bfloat16 [1024, 16384], P(None, ('row', 'col')), may hold values from -0.046875 to 0.046875
- screening: bfloat16 [4, 16384, 16384], P(None, 'row', 'col'), may hold values from -6 to 6
- qp_energy: float32 [8], replicated, may hold values from -0.5 to 0.5
- band_energy: float32 [2048], replicated, may hold values from -2 to 2
- band_index: int32 [128], replicated, may hold values from 0 to 2047
- nodes: float32 [4], replicated, may hold values from 0.1 to 2
- node_weights: float32 [4], replicated, may hold values from 0.05 to 1
Outputs:
- contrib: float32 [8, 128], replicated
- sigma: float32 [8], replicated
All inputs are finite; a program needn't handle non-finite values.
Results may differ from a plain program's by a relative error of at most 0.0003.
Values may be sent and summed in bfloat16 or wider, within the bound.
A program may use at most 128 MiB of HBM per device.

v0:
```python
import jax
import jax.numpy as jnp
from jax import lax
from jax.sharding import PartitionSpec as P


def broadcast(block, axis, holder):
    block = jnp.where(lax.axis_index(axis) == holder, block, jnp.zeros_like(block))
    return lax.psum(block, axis)


def shards(pair_states, screening, qp_energy, band_energy, band_index, nodes, node_weights):
    width = screening.shape[2]
    panel = lax.all_gather(pair_states, "col", axis=1, tiled=True)
    images = jnp.einsum("pg,fgc->fpc", panel, screening, preferred_element_type=jnp.float32)
    ratio = lax.axis_size("col") // lax.axis_size("row")
    column = lax.axis_index("col")
    offset = column % ratio * width
    own_piece = lax.dynamic_slice_in_dim(panel, offset, width, 1)
    col_states = broadcast(own_piece, "row", column // ratio)
    partial_value = jnp.sum(images * col_states.astype(jnp.float32)[None, :, :], axis=2)
    table = lax.broadcasted_iota(jnp.int32, (band_index.shape[0], band_energy.shape[0]), 1)
    chosen = jnp.sum(
        jnp.where(band_index[:, None] == table, band_energy[None, :], jnp.float32(0.0)), axis=1
    )
    gap = (qp_energy[:, None] - chosen[None, :]).reshape(-1)
    factor = (
        node_weights[:, None]
        * gap[None, :]
        / (gap[None, :] * gap[None, :] + nodes[:, None] * nodes[:, None])
    )
    flat = lax.psum(jnp.sum(factor * partial_value, axis=0), ("row", "col"))
    contrib = flat.reshape(qp_energy.shape[0], band_index.shape[0])
    sigma = jnp.sum(contrib, axis=1)
    return (contrib, sigma)


def solution(mesh):
    in_specs = (P(None, ("row", "col")), P(None, "row", "col"), P(), P(), P(), P(), P())
    out_specs = (P(), P())
    return jax.shard_map(shards, mesh=mesh, in_specs=in_specs, out_specs=out_specs, check_vma=False)
```

profile of v0, /device:TPU:0, one launch (start us, length us, event | category | flops | bytes accessed | tf_op | source)
XLA Modules:
  0.0 333.2 jit_solution(11457879454940917840)
XLA Ops:
  7.2 0.0 copy-start.8
  7.2 0.0 copy-start.3
  7.2 0.0 copy-start.5
  7.2 0.0 copy-start.4
  7.2 0.0 all-gather.2.cloned.1.call-start
  7.2 0.7 all-gather.2.cloned.1.call-update
  7.9 0.0 all-reduce.2.cloned.1.call-start
  8.0 86.4 %all-gather.2.cloned.1.call-done = bf16[1024,4096]{1,0:T(8,128)(2,1)} async-done(((bf16[1024,512]{1,0:T(8,128)(2,1)}), bf16[1024,4096]{1,0:T(8,128)(2,1)}) %all-gather.2.cloned.1.call-update) | async-done | bytes 8388624 | tf_op jit(solution)/shard_map/all_gather | solution.py:14
  94.4 5.5 %dynamic-slice_select_fusion = bf16[1024,2048]{1,0:T(8,128)(2,1)} fusion(bf16[1024,4096]{1,0:T(8,128)(2,1)} %all-gather.2.cloned.1.call-done, s32[]{:T(128)S(6)} %select_n.30, pred[]{:T(512)S(6)} %eq.15), kind=kLoop, calls=%fused_computation.3 | loop fusion | flops 2097152 | bytes 8388613 | tf_op jit(solution)/shard_map/jit(_where)/select_n | solution.py:8
  99.9 0.0 all-reduce.2.cloned.1.call-update
  99.9 0.0 copy-done.8
  99.9 0.5 mul.43
  100.4 0.0 copy-done.3
  100.4 0.0 copy-done.5
  100.4 0.2 select_reduce_fusion
  100.7 0.0 copy-done.4
  100.7 0.7 fusion.2
  101.4 0.7 subtract_bitcast_fusion
  102.0 100.2 %all-reduce.2.cloned.1.call-done = bf16[1024,2048]{1,0:T(8,128)(2,1)} async-done(((bf16[1024,2048]{1,0:T(8,128)(2,1)}), bf16[1024,2048]{1,0:T(8,128)(2,1)}) %all-reduce.2.cloned.1.call-update) | async-done | bytes 4194320 | tf_op jit(solution)/shard_map/psum | solution.py:9
  202.2 6.9 %copy.12 = f32[1024,2048]{0,1:T(8,128)} copy(bf16[1024,2048]{1,0:T(8,128)(2,1)} %all-reduce.2.cloned.1.call-done) | data formatting | bytes 12582912 | tf_op jit(solution)/shard_map/convert_element_type | solution.py:21
  209.1 77.2 %fusion = f32[4,1024]{1,0:T(4,128)S(1)} fusion(bf16[4,4096,2048]{2,1,0:T(8,128)(2,1)} %param.8, f32[1024,2048]{0,1:T(8,128)} %copy.12, bf16[1024,4096]{1,0:T(8,128)(2,1)} %all-gather.2.cloned.1.call-done), kind=kOutput, calls=%fused_computation.1 | convolution fusion | flops 68736253952 | bytes 83902464 | tf_op jit(solution)/shard_map/pg,fgc->fpc/dot_general | solution.py:15
  286.3 0.1 multiply_reduce_fusion
  286.4 39.3 %psum.15 = f32[8,128]{1,0:T(8,128)S(1)} all-reduce(f32[8,128]{1,0:T(8,128)S(1)} %bitcast.13), channel_id=1, replica_groups=mesh['row'=4,'col'=8] {'row','col'}, use_global_device_ids=true, to_apply=%region_4.5 | all-reduce | flops 1024 | bytes 8192 | tf_op jit(solution)/shard_map/psum | solution.py:32
  325.8 0.6 reduce_sum.39
  (10 shorter events, 0.0 us)
Async XLA Ops:
  7.2 92.8 %copy-start.8 = (f32[4]{0:T(128)S(1)}, f32[4]{0:T(128)}, u32[]{:S(2)}) copy-start(f32[4]{0:T(128)} %param.12) | copy-start | bytes 52
  7.2 93.3 %copy-start.3 = (f32[2048]{0:T(1024)S(1)}, f32[2048]{0:T(1024)}, u32[]{:S(2)}) copy-start(f32[2048]{0:T(1024)} %param.10) | copy-start | bytes 24580
  7.2 93.3 %copy-start.5 = (s32[128]{0:T(128)S(1)}, s32[128]{0:T(128)}, u32[]{:S(2)}) copy-start(s32[128]{0:T(128)} %param.11) | copy-start | bytes 1540
  7.2 93.5 %copy-start.4 = (f32[8]{0:T(128)S(1)}, f32[8]{0:T(128)}, u32[]{:S(2)}) copy-start(f32[8]{0:T(128)} %param.9) | copy-start | bytes 100
  7.2 87.2 %all-gather.2.cloned.1.call-start = ((), (), s32[]{:S(2)}) async-start(), calls=%async_computation | async-start | bytes 9437184 | tf_op jit(solution)/shard_map/all_gather | solution.py:14
  7.9 194.2 %all-reduce.2.cloned.1.call-start = ((), (), s32[]{:S(2)}) async-start(), calls=%async_computation.1 | async-start | bytes 8388608 | tf_op jit(solution)/shard_map/psum | solution.py:9
  209.0 77.3 %copy-start.1 = (f32[1024]{0:T(1024)S(1)}, f32[1024]{0:T(1024)}, u32[]{:S(2)}) copy-start(f32[1024]{0:T(1024)} %fusion.2) | copy-start | bytes 12292
  209.0 77.3 %copy-start.2 = (f32[1024]{0:T(1024)S(1)}, f32[1024]{0:T(1024)}, u32[]{:S(2)}) copy-start(f32[1024]{0:T(1024)} %subtract_bitcast_fusion) | copy-start | bytes 12292
  209.0 77.3 %copy-start.6 = (f32[4]{0:T(128)S(1)}, f32[4]{0:T(128)}, u32[]{:S(2)}) copy-start(f32[4]{0:T(128)} %param.13) | copy-start | bytes 52
  209.0 77.3 %copy-start.7 = (f32[4]{0:T(128)S(1)}, f32[4]{0:T(128)}, u32[]{:S(2)}) copy-start(f32[4]{0:T(128)} %mul.43) | copy-start | bytes 52
  325.8 0.6 copy-start
Sparse Core Ops, SparseCore 0:
  9.6 84.7 all-gather.1
  100.0 102.0 all-reduce.1
where the time goes:
time: 334 us; the launch traced here: 333 us
  waiting for transfers between devices  187 us (56%)
  matrix products  77.2 us (23%)
  blocking collectives  39.3 us (12%)
  between operations  14.2 us (4%)
  other arithmetic  8.28 us (2%)
  local copies, waits for them, and re-layouts  6.9 us (2%)
    psum x1, waiting for transfers between devices, broadcast(): return lax.psum(block, axis)  100 us
    all_gather x1, waiting for transfers between devices, shards(): panel = lax.all_gather(pair_states, 'col', axis=1, tiled=True)  86.4 us
    dot_general x1, matrix products, shards(): jnp.einsum('pg,fgc->fpc', panel, screening, preferred_element_type=jnp.fl...  77.2 us
    psum x1, blocking collectives, shards(): flat = lax.psum(jnp.sum(factor * partial_value, axis=0), ('row', 'col'))  39.3 us
    convert_element_type x1, local copies, waits for them, and re-layouts, shards(): col_states.astype(jnp.float32)[None, :, :]  6.86 us
  transfers between devices with their start and end apart: 2, of which 2 were waited for; matrix products, arithmetic and copies ran while one was open for 1% of the time, Pallas kernels for 0%

commit v1 on v0

--- a/solution.py
+++ b/solution.py
@@ -1,7 +1,358 @@
+import functools
+
 import jax
 import jax.numpy as jnp
 from jax import lax
+from jax.experimental import pallas as pl
+from jax.experimental.pallas import tpu as pltpu
 from jax.sharding import PartitionSpec as P
+
+MESH = pl.DeviceIdType.MESH
+CORES = 2
+
+
+def orders(chips):
+    table = []
+    for here in range(chips):
+        steps = [(here, 0), (here, 1)]
+        for reach in range(1, chips):
+            near = [other for other in (here - reach, here + reach) if 0 <= other < chips]
+            steps += [(other, 0) for other in near] + [(other, 1) for other in near]
+        table.append(steps)
+    return table
+
+
+def relay_steps(chips):
+    return [2 * reach for reach in range(1, chips)]
+
+
+def pick(table, row, column):
+    value = jnp.int32(0)
+    for i, line in enumerate(table):
+        for j, entry in enumerate(line):
+            if entry:
+                value = jnp.where((row == i) & (column == j), jnp.int32(entry), value)
+    return value
+
+
+def kernel(
+    rows, columns, own_ref, w_ref, factor_ref, out_ref,
+    panel, cols, acc, tiles, quad, near_sum, far_sum,
+    tile_sem, own_sem, send_sem, recv_sem, col_send, col_recv, near_send, near_recv, far_send, far_recv,
+):
+    row, column = lax.axis_index("row"), lax.axis_index("col")
+    chips = columns // CORES
+    chip, core = column // CORES, column % CORES
+    partner = column + 1 - 2 * core
+    freqs, _, width = w_ref.shape
+    depth = own_ref.shape[1]
+    pieces = width // depth
+    pairs = own_ref.shape[0]
+    table = orders(chips)
+    steps = columns
+
+    def at(r, c):
+        return {"row": r, "col": c}
+
+    barrier = pltpu.get_barrier_semaphore()
+    linear = row * columns + column
+    to_row, to_col = linear % pieces, linear // pieces
+    stays = (to_row == row) & (to_col == column)
+    first = row * 0 + column * pieces + row
+    from_row, from_col = first // columns, first % columns
+    for other in range(1, columns):
+        pl.semaphore_signal(barrier, inc=1, device_id=at(row, (column + other) % columns), device_id_type=MESH)
+    for other in range(1, rows):
+        pl.semaphore_signal(barrier, inc=1, device_id=at((row + other) % rows, column), device_id_type=MESH)
+
+    @pl.when(jnp.logical_not(stays))
+    def _():
+        pl.semaphore_signal(barrier, inc=1, device_id=at(to_row, to_col), device_id_type=MESH)
+        pl.semaphore_signal(barrier, inc=1, device_id=at(from_row, from_col), device_id_type=MESH)
+
+    def slot_of(step):
+        source = pick([[s[0] for s in line] for line in table], chip, step)
+        other = pick([[s[1] for s in line] for line in table], chip, step)
+        return source * CORES + jnp.where(other == 1, 1 - core, core)
+
+    def tile_copy(index):
+        step, freq = index // freqs, index % freqs
+        lines = pl.ds(pl.multiple_of(slot_of(step) * depth, depth), depth)
+        spot = index % tiles.shape[0]
+        return pltpu.make_async_copy(w_ref.at[freq, lines, :], tiles.at[spot], tile_sem.at[spot])
+
+    ahead = tiles.shape[0] - 1
+    for index in range(ahead):
+        tile_copy(index).start()
+    own_copy = pltpu.make_async_copy(own_ref, panel.at[column], own_sem)
+    own_copy.start()
+
+    pl.semaphore_wait(barrier, columns + rows - 2 + jnp.where(stays, 0, 2))
+    own_copy.wait()
+
+    def pass_on(source, way):
+        slot = source * CORES + core
+        target = [column + CORES, column - CORES, partner][way]
+        return pltpu.make_async_remote_copy(
+            src_ref=panel.at[slot], dst_ref=panel.at[slot], send_sem=send_sem.at[way, source],
+            recv_sem=recv_sem.at[slot], device_id=at(row, target), device_id_type=MESH,
+        )
+
+    def goes(source, way):
+        if way == 0:
+            return (source <= chip) & (chip < chips - 1)
+        return (source >= chip) & (chip > 0)
+
+    def forward(source):
+        for way in (0, 1):
+
+            @pl.when(goes(source, way))
+            def _():
+                pass_on(source, way).start()
+
+        pass_on(source, 2).start()
+
+    def arrive(slot):
+        pltpu.make_async_copy(panel.at[slot], panel.at[slot], recv_sem.at[slot]).wait()
+
+    def col_first():
+        return pltpu.make_async_remote_copy(
+            src_ref=panel.at[column], dst_ref=cols.at[to_row], send_sem=col_send.at[0],
+            recv_sem=col_recv.at[to_row], device_id=at(to_row, to_col), device_id_type=MESH,
+        )
+
+    def col_local():
+        return pltpu.make_async_copy(panel.at[column], cols.at[row], col_recv.at[row])
+
+    def col_next(other):
+        return pltpu.make_async_remote_copy(
+            src_ref=cols.at[row], dst_ref=cols.at[row], send_sem=col_send.at[other],
+            recv_sem=col_recv.at[row], device_id=at((row + other) % rows, column), device_id_type=MESH,
+        )
+
+    def col_arrive(slot):
+        pltpu.make_async_copy(cols.at[slot], cols.at[slot], col_recv.at[slot]).wait()
+
+    forward(chip)
+
+    @pl.when(jnp.logical_not(stays))
+    def _():
+        col_first().start()
+
+    @pl.when(stays)
+    def _():
+        col_local().start()
+
+    def product(slot, spot, piece):
+        return jnp.dot(
+            panel[slot], tiles[spot, :, pl.ds(pl.multiple_of(piece * depth, depth), depth)],
+            preferred_element_type=jnp.float32,
+        )
+
+    def each(step, work):
+        slot = slot_of(step)
+
+        @pl.loop(0, freqs)
+        def _(freq):
+            index = step * freqs + freq
+            spot = index % tiles.shape[0]
+
+            @pl.when(index + ahead < steps * freqs)
+            def _():
+                tile_copy(index + ahead).start()
+
+            tile_copy(index).wait()
+
+            @pl.loop(0, pieces)
+            def _(piece):
+                work(freq, piece, product(slot, spot, piece))
+
+    def at_piece(piece):
+        return pl.ds(pl.multiple_of(piece * depth, depth), depth)
+
+    def store(freq, piece, value):
+        acc[freq, :, at_piece(piece)] = value
+
+    def add(freq, piece, value):
+        acc[freq, :, at_piece(piece)] += value
+
+    def close(freq, piece, value):
+        total = (acc[freq, :, at_piece(piece)] + value) * cols[piece].astype(jnp.float32)
+        part = total[:, :128]
+        for lane in range(128, depth, 128):
+            part = part + total[:, lane : lane + 128]
+
+        @pl.when(piece == 0)
+        def _():
+            quad[freq] = part
+
+        @pl.when(piece > 0)
+        def _():
+            quad[freq] += part
+
+    each(0, store)
+
+    def sides(reach, work):
+        for source in (chip - reach, chip + reach):
+
+            @pl.when((source >= 0) & (source < chips))
+            def _():
+                work(source)
+
+    def prepare(step):
+        for reach, when in enumerate(relay_steps(chips), 1):
+
+            @pl.when(step == when)
+            def _():
+                def one(source):
+                    arrive(source * CORES + core)
+                    forward(source)
+
+                sides(reach, one)
+
+        @pl.when(step == COL_STEP)
+        def _():
+            col_arrive(row)
+            for other in range(1, rows):
+                col_next(other).start()
+
+        slot = slot_of(step)
+
+        @pl.when(slot % CORES != core)
+        def _():
+            arrive(slot)
+
+    @pl.loop(1, steps - 1)
+    def _(step):
+        prepare(step)
+        each(step, add)
+
+    prepare(steps - 1)
+    for other in range(1, rows):
+        col_arrive((row + other) % rows)
+    each(steps - 1, close)
+
+    bands = pairs // 128
+    lines = []
+    for band in range(bands):
+        line = jnp.zeros((1, 128), jnp.float32)
+        for freq in range(freqs):
+            turned = quad[freq, pl.ds(band * 128, 128), :].T
+            line = line + jnp.sum(turned, axis=0, keepdims=True) * factor_ref[freq, pl.ds(band, 1), :]
+        lines.append(line)
+    near_sum[column] = jnp.concatenate(lines, axis=0)
+
+    def near(other):
+        return pltpu.make_async_remote_copy(
+            src_ref=near_sum.at[column], dst_ref=near_sum.at[column], send_sem=near_send.at[other],
+            recv_sem=near_recv.at[column], device_id=at(row, (column + other) % columns), device_id_type=MESH,
+        )
+
+    def far(other):
+        return pltpu.make_async_remote_copy(
+            src_ref=far_sum.at[row], dst_ref=far_sum.at[row], send_sem=far_send.at[other],
+            recv_sem=far_recv.at[row], device_id=at((row + other) % rows, column), device_id_type=MESH,
+        )
+
+    for other in range(1, columns):
+        near(other).start()
+    for other in range(1, columns):
+        slot = (column + other) % columns
+        pltpu.make_async_copy(near_sum.at[slot], near_sum.at[slot], near_recv.at[slot]).wait()
+    total = near_sum[0]
+    for slot in range(1, columns):
+        total = total + near_sum[slot]
+    far_sum[row] = total
+    for other in range(1, rows):
+        far(other).start()
+    for other in range(1, rows):
+        slot = (row + other) % rows
+        pltpu.make_async_copy(far_sum.at[slot], far_sum.at[slot], far_recv.at[slot]).wait()
+    total = far_sum[0]
+    for slot in range(1, rows):
+        total = total + far_sum[slot]
+    out_ref[...] = total
+
+    def sent(source):
+        for way in (0, 1):
+
+            @pl.when(goes(source, way))
+            def _():
+                pass_on(source, way).wait_send()
+
+        pass_on(source, 2).wait_send()
+
+    for source in range(chips):
+        sent(source)
+
+    @pl.when(jnp.logical_not(stays))
+    def _():
+        col_first().wait_send()
+
+    for other in range(1, rows):
+        col_next(other).wait_send()
+        far(other).wait_send()
+    for other in range(1, columns):
+        near(other).wait_send()
+
+
+def weights(qp_energy, band_energy, band_index, nodes, node_weights):
+    table = lax.broadcasted_iota(jnp.int32, (band_index.shape[0], band_energy.shape[0]), 1)
+    chosen = jnp.sum(
+        jnp.where(band_index[:, None] == table, band_energy[None, :], jnp.float32(0.0)), axis=1
+    )
+    gap = (qp_energy[:, None] - chosen[None, :])[None]
+    return node_weights[:, None, None] * gap / (gap * gap + (nodes * nodes)[:, None, None])
+
+
+COL_STEP = 3
+
+
+def fused(pair_states, screening, qp_energy, band_energy, band_index, nodes, node_weights):
+    rows, columns = lax.axis_size("row"), lax.axis_size("col")
+    pairs, depth = pair_states.shape
+    freqs, _, width = screening.shape
+    factor = weights(qp_energy, band_energy, band_index, nodes, node_weights)
+    shape = (qp_energy.shape[0], band_index.shape[0])
+    dma = pltpu.SemaphoreType.DMA
+    contrib = pl.pallas_call(
+        functools.partial(kernel, rows, columns),
+        out_shape=jax.ShapeDtypeStruct(shape, jnp.float32),
+        in_specs=[
+            pl.BlockSpec(memory_space=pl.ANY),
+            pl.BlockSpec(memory_space=pl.ANY),
+            pl.BlockSpec(memory_space=pltpu.VMEM),
+        ],
+        out_specs=pl.BlockSpec(memory_space=pltpu.VMEM),
+        scratch_shapes=[
+            pltpu.VMEM((columns, pairs, depth), jnp.bfloat16),
+            pltpu.VMEM((width // depth, pairs, depth), jnp.bfloat16),
+            pltpu.VMEM((freqs, pairs, width), jnp.float32),
+            pltpu.VMEM((3, depth, width), jnp.bfloat16),
+            pltpu.VMEM((freqs, pairs, 128), jnp.float32),
+            pltpu.VMEM((columns,) + shape, jnp.float32),
+            pltpu.VMEM((rows,) + shape, jnp.float32),
+            dma((3,)),
+            dma,
+            dma((3, columns // CORES)),
+            dma((columns,)),
+            dma((rows,)),
+            dma((rows,)),
+            dma((columns,)),
+            dma((columns,)),
+            dma((rows,)),
+            dma((rows,)),
+        ],
+        compiler_params=pltpu.CompilerParams(
+            collective_id=0, has_side_effects=True, vmem_limit_bytes=67043328
+        ),
+        cost_estimate=pl.CostEstimate(
+            flops=2 * freqs * pairs * columns * depth * width,
+            bytes_accessed=freqs * columns * depth * width * 2,
+            transcendentals=0,
+        ),
+    )(pair_states, screening, factor)
+    return contrib, jnp.sum(contrib, axis=1)
 
 
 def broadcast(block, axis, holder):
@@ -35,7 +386,17 @@
     return (contrib, sigma)
 
 
+def step(pair_states, screening, *others):
+    rows, columns = lax.axis_size("row"), lax.axis_size("col")
+    pairs, depth = pair_states.shape
+    freqs, _, width = screening.shape
+    held = pairs * (columns * depth * 2 + width * 2 + freqs * width * 4 + freqs * 512) + 3 * depth * width * 2
+    fits = depth % 128 == 0 and width == rows * depth and columns % CORES == 0 and held < 60 * 2**20
+    fits = fits and others[2].shape[0] == 128 and columns >= 2 * CORES
+    return (fused if fits else shards)(pair_states, screening, *others)
+
+
 def solution(mesh):
     in_specs = (P(None, ("row", "col")), P(None, "row", "col"), P(), P(), P(), P(), P())
     out_specs = (P(), P())
-    return jax.shard_map(shards, mesh=mesh, in_specs=in_specs, out_specs=out_specs, check_vma=False)
+    return jax.shard_map(step, mesh=mesh, in_specs=in_specs, out_specs=out_specs, check_vma=False)

time: 334 us -> 185 us (0.55)
  waiting for transfers between devices: 187 us -> 0 us
  Pallas kernels: 0 us -> 178 us
  matrix products: 77.2 us -> 0 us
  blocking collectives: 39.3 us -> 0 us
  between operations: 14.2 us -> 0.64 us
  local copies, waits for them, and re-layouts: 6.9 us -> 1.26 us
    pallas_call x0 -> x1, Pallas kernels: none -> 178 us  [fused(): pl.pallas_call(functools.partial(kernel, rows, columns), out_shape=jax.Sh...]
    psum x1 -> x0, waiting for transfers between devices: 100 us -> none  [broadcast(): return lax.psum(block, axis)]
    all_gather x1 -> x0, waiting for transfers between devices: 86.4 us -> none  [shards(): panel = lax.all_gather(pair_states, 'col', axis=1, tiled=True)]
    dot_general x1 -> x0, matrix products: 77.2 us -> none  [shards(): jnp.einsum('pg,fgc->fpc', panel, screening, preferred_element_type=jnp.fl...]
    psum x1 -> x0, blocking collectives: 39.3 us -> none  [shards(): flat = lax.psum(jnp.sum(factor * partial_value, axis=0), ('row', 'col'))]
    convert_element_type x1 -> x0, local copies, waits for them, and re-layouts: 6.86 us -> none  [shards(): col_states.astype(jnp.float32)[None, :, :]]
    select_n x1 -> x0, other arithmetic: 5.48 us -> none  [broadcast(): jnp.where(lax.axis_index(axis) == holder, block, jnp.zeros_like(block))]
  transfers between devices with their start and end apart: 2 -> 0, of which waited for: 2 -> 0; matrix products, arithmetic and copies ran while one was open for 1% -> 0% of each run, Pallas kernels for 0% -> 0%
where the time goes in v1:
time: 185 us
  Pallas kernels  178 us (96%)
  other arithmetic  5.04 us (3%)
    pallas_call x1, Pallas kernels, fused(): pl.pallas_call(functools.partial(kernel, rows, columns), out_shape=jax.Sh...  178 us

profile of v1, /device:TPU:0, one launch (start us, length us, event | category | flops | bytes accessed | tf_op | source)
XLA Modules:
  0.0 184.8 jit_solution(17285373552223058375)
XLA Ops:
  0.6 0.9 select_reduce_fusion
  1.6 0.7 mul.28
  2.3 0.7 broadcast_subtract_fusion
  3.0 1.3 add_divide_fusion.factor_ref
  4.4 177.9 %shard_map.86 = f32[8,128]{1,0:T(8,128)} custom-call(bf16[1024,512]{1,0:T(8,128)(2,1)} %own_ref.1, bf16[4,4096,2048]{2,1,0:T(8,128)(2,1)} %w_ref.1, f32[4,8,128]{2,1,0:T(8,128)} %add_divide_fusion.factor_ref), custom_call_target="tpu_custom_call" | custom-call | flops 68719476736 | bytes 67108864 | tf_op jit(solution)/shard_map/pallas_call | solution.py:318
  182.2 1.3 reduce_sum.19
  183.5 1.3 copy.10
